TPU v7x, 32 devices: a whole 2x2x4 slice. The times are simulated.
32 devices in a mesh: dp: 4 (over z), tensor: 8 (over y, x, core).
Axes of the slice: x: 2, y: 2, z: 4, core: 2. Of those that a mesh axis runs over, the one named last changes fastest.
Arguments:
- gradient: bfloat16 [4, 2560, 8192], P('dp', None, 'tensor'), may hold values from -6 to 6
- feedback: float32 [4, 2560, 8192], P('dp', None, 'tensor'), may hold values from -4 to 4
- q_start: float32 [8192, 32], P('tensor'), may hold values from -6 to 6
Outputs:
- p_factor: float32 [2560, 32], P('tensor')
- q_factor: float32 [8192, 32], P('tensor')
- decoded: float32 [2560, 8192], P(None, 'tensor')
- residual: float32 [4, 2560, 8192], P('dp', None, 'tensor')
All inputs are finite; a program needn't handle non-finite values.
Results may differ from a plain program's by a relative error of at most 0.0003.
Values sent between devices are 32-bit elements; how exact they have to be, the bound alone decides.
A program may use at most 64 MiB of HBM per device.

v0:
```python
import jax
import jax.numpy as jnp
from jax import lax
from jax.sharding import PartitionSpec as P


def orthonormal(p_sum, gram_matrix):
    factor_low = jnp.linalg.cholesky(gram_matrix)
    return jax.scipy.linalg.solve_triangular(factor_low, p_sum.T, lower=True).T


def local(gradient, feedback, q_start):
    high = lax.Precision.HIGHEST
    merged = gradient[0].astype(jnp.float32) + feedback[0]
    row_block = lax.psum_scatter(
        jnp.dot(merged, q_start, precision=high), "tensor", scatter_dimension=0, tiled=True
    )
    row_block = lax.psum(row_block, "dp")
    gram_matrix = lax.psum(jnp.dot(row_block.T, row_block, precision=high), "tensor")
    p_factor = orthonormal(row_block, gram_matrix)
    basis_all = lax.all_gather(p_factor, "tensor", axis=0, tiled=True)
    q_local = lax.dot_general(merged, basis_all, (((0,), (0,)), ((), ())), precision=high)
    q_factor = lax.psum(q_local, "dp") / lax.axis_size("dp")
    decoded = jnp.dot(basis_all, q_factor.T, precision=high)
    residual = merged - decoded
    return (p_factor, q_factor, decoded, residual[None])


def solution(mesh):
    in_specs = (P("dp", None, "tensor"), P("dp", None, "tensor"), P("tensor", None))
    out_specs = (P("tensor", None), P("tensor", None), P(None, "tensor"), P("dp", None, "tensor"))
    return jax.shard_map(local, mesh=mesh, in_specs=in_specs, out_specs=out_specs, check_vma=False)
```

profile of v0, /device:TPU:0, one launch (start us, length us, event | category | flops | bytes accessed | tf_op | source)
XLA Modules:
  0.0 192.3 jit_solution(12324662725646355803)
XLA Ops:
  7.2 0.0 copy-start
  7.2 0.0 reduce-scatter.4.cloned.1.call-start
  7.2 0.8 copy-done
  8.1 12.6 %fusion.2 = f32[2560,32]{1,0:T(8,128)} fusion(f32[1024,32]{0,1:T(8,128)S(1)} %copy-done, f32[1,2560,1024]{2,1,0:T(8,128)} %param.4, bf16[1,2560,1024]{2,1,0:T(8,128)(2,1)} %param.3), kind=kOutput, calls=%fused_computation.3 | convolution fusion | flops 1011875840 | bytes 16187392
  20.7 0.0 reduce-scatter.4.cloned.1.call-update
  20.7 0.0 all-reduce.2.cloned.1.call-start
  20.8 40.0 %reduce-scatter.4.cloned.1.call-done = f32[320,32]{1,0:T(8,128)} async-done(((f32[2560,32]{1,0:T(8,128)}), f32[320,32]{1,0:T(8,128)}) %reduce-scatter.4.cloned.1.call-update) | async-done | bytes 40976
  60.8 1.0 copy.17
  61.8 19.5 %psum.21 = f32[320,32]{0,1:T(8,128)S(1)} all-reduce(f32[320,32]{0,1:T(8,128)S(1)} %copy.17), channel_id=1, replica_groups=mesh['dp'=4,'tensor'=8] {'dp'}, use_global_device_ids=true, to_apply=%region_1.0 | all-reduce | flops 10240 | bytes 81920 | tf_op jit(solution)/shard_map/psum | solution.py:18
  81.3 0.2 fusion.9
  81.5 22.3 %psum.22 = f32[32,32]{0,1:T(8,128)S(1)} all-reduce(f32[32,32]{0,1:T(8,128)S(1)} %fusion.9), channel_id=1, replica_groups=mesh['dp'=4,'tensor'=8] {'tensor'}, use_global_device_ids=true, to_apply=%region_2.0 | all-reduce | flops 1024 | bytes 8192 | tf_op jit(solution)/shard_map/psum | solution.py:19
  103.8 0.1 copy.13
  103.9 2.9 %cholesky.16 = f32[32,32]{1,0:T(8,128)S(1)} custom-call(f32[32,32]{1,0:T(8,128)S(1)} %fusion.8), custom_call_target="Cholesky" | custom-call | tf_op jit(solution)/shard_map/jit(cholesky)/cholesky | solution.py:8
  106.8 0.6 compare_reduce_fusion
  107.5 0.7 fusion.5
  108.1 2.4 %custom-call.7 = f32[1,32,32]{1,2,0:T(8,128)S(1)} custom-call(f32[1,32,32]{2,1,0:T(8,128)S(1)} %fusion.5), custom_call_target="InvertDiagBlocksLowerTriangular" | custom-call | tf_op jit(solution)/shard_map/jit(_solve_triangular)/triangular_solve | solution.py:9
  110.6 0.3 fusion.6
  110.9 0.0 copy-start.3
  110.9 9.6 %all-gather = f32[8,320,32]{1,2,0:T(8,128)S(1)} all-gather(f32[1,320,32]{1,2,0:T(8,128)S(1)} %bitcast.32), channel_id=1, replica_groups=mesh['dp'=4,'tensor'=8] {'tensor'}, dimensions={0}, use_global_device_ids=true | all-gather | bytes 368640 | tf_op jit(solution)/shard_map/all_gather | solution.py:21
  120.4 0.2 copy.14
  120.7 0.1 reshape.21
  120.8 11.0 %fusion = f32[1024,32]{0,1:T(8,128)} fusion(f32[2560,32]{0,1:T(8,128)S(1)} %reshape.21, f32[1,2560,1024]{2,1,0:T(8,128)} %param.4, bf16[1,2560,1024]{2,1,0:T(8,128)(2,1)} %param.3), kind=kOutput, calls=%fused_computation.1 | convolution fusion | flops 1011875840 | bytes 16187392 | tf_op jit(solution)/shard_map/dot_general | solution.py:22
  131.8 0.0 all-reduce.2.cloned.1.call-update
  131.8 32.1 %all-reduce.2.cloned.1.call-done = f32[1024,32]{0,1:T(8,128)} async-done(((f32[1024,32]{0,1:T(8,128)}), f32[1024,32]{0,1:T(8,128)}) %all-reduce.2.cloned.1.call-update) | async-done | bytes 131088 | tf_op jit(solution)/shard_map/psum | solution.py:23
  163.9 0.9 broadcast_multiply_fusion
  164.8 0.0 copy-start.2
  164.8 0.0 slice-start.1
  164.8 8.5 %fusion.10 = f32[2560,1024]{1,0:T(8,128)S(1)} fusion(f32[2560,32]{0,1:T(8,128)S(1)} %reshape.21, f32[1024,32]{0,1:T(8,128)S(1)} %broadcast_multiply_fusion), kind=kOutput, calls=%fused_computation.19 | convolution fusion | flops 1006632960 | bytes 10944512 | tf_op jit(solution)/shard_map/dot_general | solution.py:24
  173.3 0.0 copy-done.3
  173.4 0.0 copy-start.1
  173.4 12.1 %fusion.4 = f32[1,2560,1024]{2,1,0:T(8,128)} fusion(f32[2560,1024]{1,0:T(8,128)S(1)} %fusion.10, f32[1,2560,1024]{2,1,0:T(8,128)} %param.4, bf16[1,2560,1024]{2,1,0:T(8,128)(2,1)S(1)} %bitcast.31), kind=kLoop, calls=%fused_computation.5 | loop fusion | flops 7864320 | bytes 36700160 | tf_op jit(solution)/shard_map/broadcast_in_dim | solution.py:26
  185.5 0.0 copy-done.1
  (7 shorter events, 0.0 us)
Async XLA Ops:
  7.2 0.9 copy-start
  7.2 53.6 %reduce-scatter.4.cloned.1.call-start = ((), (), s32[]{:S(2)}) async-start(), calls=%async_computation.2 | async-start | bytes 1474560
  20.7 143.1 %all-reduce.2.cloned.1.call-start = ((), (), s32[]{:S(2)}) async-start(), calls=%async_computation.1 | async-start | bytes 262144 | tf_op jit(solution)/shard_map/psum | solution.py:23
  110.9 62.5 %copy-start.3 = (f32[320,32]{0,1:T(8,128)}, f32[320,32]{0,1:T(8,128)S(1)}, u32[]{:S(2)}) copy-start(f32[320,32]{0,1:T(8,128)S(1)} %fusion.6) | copy-start | bytes 122884
  131.8 41.6 %slice-start = ((s8[5242880]{0:T(1024)(128)(4,1)}), s8[1048576]{0:T(1024)(128)(4,1)S(1)}, s32[]{:S(2)}) async-start(s8[5242880]{0:T(1024)(128)(4,1)} %bitcast.30), calls=%async_computation.3 | async-start | bytes 2097152
  164.8 20.7 %copy-start.2 = (f32[1024,32]{0,1:T(8,128)}, f32[1024,32]{0,1:T(8,128)S(1)}, u32[]{:S(2)}) copy-start(f32[1024,32]{0,1:T(8,128)S(1)} %broadcast_multiply_fusion) | copy-start | bytes 393220
  164.8 8.6 %slice-start.1 = ((s8[5242880]{0:T(1024)(128)(4,1)}), s8[4194304]{0:T(1024)(128)(4,1)S(1)}, s32[]{:S(2)}) async-start(s8[5242880]{0:T(1024)(128)(4,1)} %bitcast.30), calls=%async_computation.4 | async-start | bytes 8388608
  173.4 12.1 %copy-start.1 = (f32[2560,1024]{1,0:T(8,128)}, f32[2560,1024]{1,0:T(8,128)S(1)}, u32[]{:S(2)}) copy-start(f32[2560,1024]{1,0:T(8,128)S(1)} %fusion.10) | copy-start | bytes 31457284
Sparse Core Ops, SparseCore 0:
  20.9 39.8 reduce-scatter.3
  131.9 31.8 all-reduce.1
where the time goes:
time: 193 us; the launch traced here: 192 us
  waiting for transfers between devices  72.1 us (37%)
  blocking collectives  51.4 us (27%)
  matrix products  32.6 us (17%)
  other arithmetic  19.7 us (10%)
  between operations  14.2 us (7%)
  local copies, waits for them, and re-layouts  2.32 us (1%)
    unnamed x3, waiting for transfers between devices  40 us
    psum x1, waiting for transfers between devices, local(): q_factor = lax.psum(q_local, 'dp') / lax.axis_size('dp')  32.1 us
    psum x1, blocking collectives, local(): lax.psum(jnp.dot(row_block.T, row_block, precision=high), 'tensor')  22.3 us
    psum x1, blocking collectives, local(): row_block = lax.psum(row_block, 'dp')  19.5 us
    unnamed x1, matrix products  12.6 us
    broadcast_in_dim x1, other arithmetic, local(): return (p_factor, q_factor, decoded, residual[None])  12.1 us
    dot_general x1, matrix products, local(): lax.dot_general(merged, basis_all, (((0,), (0,)), ((), ())), precision=high)  11 us
    all_gather x1, blocking collectives, local(): basis_all = lax.all_gather(p_factor, 'tensor', axis=0, tiled=True)  9.56 us
  transfers between devices with their start and end apart: 2, of which 2 were waited for; matrix products, arithmetic and copies ran while one was open for 0% of the time, Pallas kernels for 0%

commit v1 on v0

--- a/solution.py
+++ b/solution.py
@@ -15,7 +15,12 @@
     row_block = lax.psum_scatter(
         jnp.dot(merged, q_start, precision=high), "tensor", scatter_dimension=0, tiled=True
     )
-    row_block = lax.psum(row_block, "dp")
+    size = lax.axis_size("dp")
+    acc, hop = (row_block, 1)
+    while hop < size:
+        acc = acc + lax.ppermute(acc, "dp", [(i, i ^ hop) for i in range(size)])
+        hop = 2 * hop
+    row_block = acc
     gram_matrix = lax.psum(jnp.dot(row_block.T, row_block, precision=high), "tensor")
     p_factor = orthonormal(row_block, gram_matrix)
     basis_all = lax.all_gather(p_factor, "tensor", axis=0, tiled=True)

time: 193 us -> 185 us (0.959)
  blocking collectives: 51.4 us -> 31.9 us
  waiting for transfers between devices: 72.1 us -> 80.5 us
  starting transfers between devices: 0.08 us -> 4.1 us
    psum x1 -> x0, blocking collectives: 19.5 us -> none  [local(): row_block = lax.psum(row_block, 'dp')]
    ppermute x0 -> x2, waiting for transfers between devices: none -> 5.18 us  [local(): acc = acc + lax.ppermute(acc, 'dp', [(i, i ^ hop) for i in range(size)])]
    ppermute x0 -> x2, starting transfers between devices: none -> 4.02 us  [local(): acc = acc + lax.ppermute(acc, 'dp', [(i, i ^ hop) for i in range(size)])]
    psum x1, waiting for transfers between devices: 32.1 us -> 35.3 us  [local(): q_factor = lax.psum(q_local, 'dp') / lax.axis_size('dp')]
  transfers between devices with their start and end apart: 2 -> 4, of which waited for: 2 -> 4; matrix products, arithmetic and copies ran while one was open for 0% -> 0% of each run, Pallas kernels for 0% -> 0%
where the time goes in v1:
time: 185 us
  waiting for transfers between devices  80.5 us (44%)
  matrix products  32.6 us (18%)
  blocking collectives  31.9 us (17%)
  other arithmetic  19.7 us (11%)
  between operations  14.2 us (8%)
  starting transfers between devices  4.1 us (2%)
  local copies, waits for them, and re-layouts  2.32 us (1%)
    unnamed x3, waiting for transfers between devices  40 us
    psum x1, waiting for transfers between devices, local(): q_factor = lax.psum(q_local, 'dp') / lax.axis_size('dp')  35.3 us
    psum x1, blocking collectives, local(): lax.psum(jnp.dot(row_block.T, row_block, precision=high), 'tensor')  22.3 us
    unnamed x1, matrix products  12.6 us
    broadcast_in_dim x1, other arithmetic, local(): return (p_factor, q_factor, decoded, residual[None])  12.1 us
    dot_general x1, matrix products, local(): lax.dot_general(merged, basis_all, (((0,), (0,)), ((), ())), precision=high)  11 us
    all_gather x1, blocking collectives, local(): basis_all = lax.all_gather(p_factor, 'tensor', axis=0, tiled=True)  9.56 us
    dot_general x1, matrix products, local(): decoded = jnp.dot(basis_all, q_factor.T, precision=high)  8.54 us
  transfers between devices with their start and end apart: 4, of which 4 were waited for; matrix products, arithmetic and copies ran while one was open for 0% of the time, Pallas kernels for 0%

profile of v1, /device:TPU:0, one launch (start us, length us, event | category | flops | bytes accessed | tf_op | source)
XLA Modules:
  0.0 185.3 jit_solution(1346196346003850608)
XLA Ops:
  7.2 0.0 copy-start
  7.2 0.0 reduce-scatter.4.cloned.1.call-start
  7.2 0.8 copy-done
  8.1 12.6 %fusion.2 = f32[2560,32]{1,0:T(8,128)} fusion(f32[1024,32]{0,1:T(8,128)S(1)} %copy-done, f32[1,2560,1024]{2,1,0:T(8,128)} %param.4, bf16[1,2560,1024]{2,1,0:T(8,128)(2,1)} %param.3), kind=kOutput, calls=%fused_computation.3 | convolution fusion | flops 1011875840 | bytes 16187392
  20.7 0.0 reduce-scatter.4.cloned.1.call-update
  20.7 0.0 all-reduce.2.cloned.1.call-start
  20.8 40.0 %reduce-scatter.4.cloned.1.call-done = f32[320,32]{1,0:T(8,128)} async-done(((f32[2560,32]{1,0:T(8,128)}), f32[320,32]{1,0:T(8,128)}) %reduce-scatter.4.cloned.1.call-update) | async-done | bytes 40976
  60.8 1.0 copy.17
  61.8 1.5 collective-permute-start
  63.3 2.6 %collective-permute-done = f32[320,32]{0,1:T(8,128)S(1)} collective-permute-done((f32[320,32]{0,1:T(8,128)S(1)}, f32[320,32]{0,1:T(8,128)S(1)}, u32[]{:S(2)}, u32[]{:S(2)}) %collective-permute-start) | collective-permute-done | bytes 40992 | tf_op jit(solution)/shard_map/ppermute | solution.py:21
  65.9 2.5 %collective-permute-start.1 = (f32[320,32]{0,1:T(8,128)S(1)}, f32[320,32]{0,1:T(8,128)S(1)}, u32[]{:S(2)}, u32[]{:S(2)}) collective-permute-start(f32[320,32]{0,1:T(8,128)S(1)} %add.32), channel_id=1, source_target_pairs={{0,16},{8,24},{16,0},{24,8},{1,17},{9,25},{17,1},{25,9},{2,18},{10... | collective-permute-start | bytes 122888 | tf_op jit(solution)/shard_map/ppermute | solution.py:21
  68.4 2.6 %collective-permute-done.1 = f32[320,32]{0,1:T(8,128)S(1)} collective-permute-done((f32[320,32]{0,1:T(8,128)S(1)}, f32[320,32]{0,1:T(8,128)S(1)}, u32[]{:S(2)}, u32[]{:S(2)}) %collective-permute-start.1) | collective-permute-done | bytes 40992 | tf_op jit(solution)/shard_map/ppermute | solution.py:21
  71.0 0.2 fusion.9
  71.2 22.3 %psum.14 = f32[32,32]{0,1:T(8,128)S(1)} all-reduce(f32[32,32]{0,1:T(8,128)S(1)} %fusion.9), channel_id=1, replica_groups=mesh['dp'=4,'tensor'=8] {'tensor'}, use_global_device_ids=true, to_apply=%region_1.0 | all-reduce | flops 1024 | bytes 8192 | tf_op jit(solution)/shard_map/psum | solution.py:24
  93.5 0.1 copy.13
  93.6 2.9 %cholesky.16 = f32[32,32]{1,0:T(8,128)S(1)} custom-call(f32[32,32]{1,0:T(8,128)S(1)} %fusion.8), custom_call_target="Cholesky" | custom-call | tf_op jit(solution)/shard_map/jit(cholesky)/cholesky | solution.py:8
  96.5 0.6 compare_reduce_fusion
  97.2 0.7 fusion.5
  97.8 2.4 %custom-call.7 = f32[1,32,32]{1,2,0:T(8,128)S(1)} custom-call(f32[1,32,32]{2,1,0:T(8,128)S(1)} %fusion.5), custom_call_target="InvertDiagBlocksLowerTriangular" | custom-call | tf_op jit(solution)/shard_map/jit(_solve_triangular)/triangular_solve | solution.py:9
  100.3 0.3 fusion.6
  100.6 9.6 %all-gather = f32[8,320,32]{1,2,0:T(8,128)S(1)} all-gather(f32[1,320,32]{1,2,0:T(8,128)S(1)} %bitcast.32), channel_id=1, replica_groups=mesh['dp'=4,'tensor'=8] {'tensor'}, dimensions={0}, use_global_device_ids=true | all-gather | bytes 368640 | tf_op jit(solution)/shard_map/all_gather | solution.py:26
  110.1 0.2 copy.14
  110.4 0.1 reshape.21
  110.5 11.0 %fusion = f32[1024,32]{0,1:T(8,128)} fusion(f32[2560,32]{0,1:T(8,128)S(1)} %reshape.21, f32[1,2560,1024]{2,1,0:T(8,128)} %param.4, bf16[1,2560,1024]{2,1,0:T(8,128)(2,1)} %param.3), kind=kOutput, calls=%fused_computation.1 | convolution fusion | flops 1011875840 | bytes 16187392 | tf_op jit(solution)/shard_map/dot_general | solution.py:27
  121.5 0.0 all-reduce.2.cloned.1.call-update
  121.5 35.3 %all-reduce.2.cloned.1.call-done = f32[1024,32]{0,1:T(8,128)} async-done(((f32[1024,32]{0,1:T(8,128)}), f32[1024,32]{0,1:T(8,128)}) %all-reduce.2.cloned.1.call-update) | async-done | bytes 131088 | tf_op jit(solution)/shard_map/psum | solution.py:28
  156.8 0.9 broadcast_multiply_fusion
  157.7 0.0 copy-start.2
  157.7 0.0 slice-start.1
  157.7 8.5 %fusion.10 = f32[2560,1024]{1,0:T(8,128)S(1)} fusion(f32[2560,32]{0,1:T(8,128)S(1)} %reshape.21, f32[1024,32]{0,1:T(8,128)S(1)} %broadcast_multiply_fusion), kind=kOutput, calls=%fused_computation.19 | convolution fusion | flops 1006632960 | bytes 10944512 | tf_op jit(solution)/shard_map/dot_general | solution.py:29
  166.3 0.0 copy-start.1
  166.3 12.1 %fusion.4 = f32[1,2560,1024]{2,1,0:T(8,128)} fusion(f32[2560,1024]{1,0:T(8,128)S(1)} %fusion.10, f32[1,2560,1024]{2,1,0:T(8,128)} %param.4, bf16[1,2560,1024]{2,1,0:T(8,128)(2,1)S(1)} %bitcast.31), kind=kLoop, calls=%fused_computation.5 | loop fusion | flops 7864320 | bytes 36700160 | tf_op jit(solution)/shard_map/broadcast_in_dim | solution.py:31
  (12 shorter events, 0.1 us)
Async XLA Ops:
  7.2 0.9 copy-start
  7.2 53.6 %reduce-scatter.4.cloned.1.call-start = ((), (), s32[]{:S(2)}) async-start(), calls=%async_computation.2 | async-start | bytes 1474560
  20.7 136.1 %all-reduce.2.cloned.1.call-start = ((), (), s32[]{:S(2)}) async-start(), calls=%async_computation.1 | async-start | bytes 262144 | tf_op jit(solution)/shard_map/psum | solution.py:28
  61.8 4.1 %collective-permute-start = (f32[320,32]{0,1:T(8,128)S(1)}, f32[320,32]{0,1:T(8,128)S(1)}, u32[]{:S(2)}, u32[]{:S(2)}) collective-permute-start(f32[320,32]{0,1:T(8,128)S(1)} %copy.17), channel_id=1, source_target_pairs={{0,8},{8,0},{16,24},{24,16},{1,9},{9,1},{17,25},{25,17},{2,10},{10... | collective-permute-start | bytes 122888 | tf_op jit(solution)/shard_map/ppermute | solution.py:21
  65.9 5.1 %collective-permute-start.1 = (f32[320,32]{0,1:T(8,128)S(1)}, f32[320,32]{0,1:T(8,128)S(1)}, u32[]{:S(2)}, u32[]{:S(2)}) collective-permute-start(f32[320,32]{0,1:T(8,128)S(1)} %add.32), channel_id=1, source_target_pairs={{0,16},{8,24},{16,0},{24,8},{1,17},{9,25},{17,1},{25,9},{2,18},{10... | collective-permute-start | bytes 122888 | tf_op jit(solution)/shard_map/ppermute | solution.py:21
  100.6 65.7 %copy-start.3 = (f32[320,32]{0,1:T(8,128)}, f32[320,32]{0,1:T(8,128)S(1)}, u32[]{:S(2)}) copy-start(f32[320,32]{0,1:T(8,128)S(1)} %fusion.6) | copy-start | bytes 122884
  121.5 44.8 %slice-start = ((s8[5242880]{0:T(1024)(128)(4,1)}), s8[1048576]{0:T(1024)(128)(4,1)S(1)}, s32[]{:S(2)}) async-start(s8[5242880]{0:T(1024)(128)(4,1)} %bitcast.30), calls=%async_computation.3 | async-start | bytes 2097152
  157.7 20.7 %copy-start.2 = (f32[1024,32]{0,1:T(8,128)}, f32[1024,32]{0,1:T(8,128)S(1)}, u32[]{:S(2)}) copy-start(f32[1024,32]{0,1:T(8,128)S(1)} %broadcast_multiply_fusion) | copy-start | bytes 393220
  157.7 8.6 %slice-start.1 = ((s8[5242880]{0:T(1024)(128)(4,1)}), s8[4194304]{0:T(1024)(128)(4,1)S(1)}, s32[]{:S(2)}) async-start(s8[5242880]{0:T(1024)(128)(4,1)} %bitcast.30), calls=%async_computation.4 | async-start | bytes 8388608
  166.3 12.1 %copy-start.1 = (f32[2560,1024]{1,0:T(8,128)}, f32[2560,1024]{1,0:T(8,128)S(1)}, u32[]{:S(2)}) copy-start(f32[2560,1024]{1,0:T(8,128)S(1)} %fusion.10) | copy-start | bytes 31457284
Sparse Core Ops, SparseCore 0:
  20.9 39.8 reduce-scatter.3
  121.6 35.1 all-reduce.1
